TPU v7x, 32 devices: a whole 2x2x4 slice. The times are simulated.
32 devices in a mesh: dp: 8 (over y, x, core), fsdp: 4 (over z).
Axes of the slice: x: 2, y: 2, z: 4, core: 2. Of those that a mesh axis runs over, the one named last changes fastest.
Arguments:
- tokens: bfloat16 [4096, 4096], P('dp'), may hold values from -6 to 6
- counts: int32 [8], P('dp'), may hold values from 256 to 512, as said below
- patch_index: int32 [4096], P('dp'), may hold values from 0 to 255
- clip_limit: float32 [], replicated, may hold values from 1024 to 8192
- norm_gain: float32 [4, 4096], replicated, may hold values from 0.25 to 1.75
- params: float32 [4, 4096, 4096], P(None, 'dp', 'fsdp'), may hold values from -0.09375 to 0.09375
- moments: float32 [4, 4096, 4096], P(None, 'dp', 'fsdp'), may hold values from -0.3 to 0.3
- seconds: float32 [4, 4096, 4096], P(None, 'dp', 'fsdp'), may hold values from 0.05 to 1
- gradients: float32 [4, 4096, 4096], P(None, 'dp', 'fsdp'), may hold values from -48 to 48
Outputs:
- params_new: float32 [4, 4096, 4096], P(None, 'dp', 'fsdp')
- moments_new: float32 [4, 4096, 4096], P(None, 'dp', 'fsdp')
- seconds_new: float32 [4, 4096, 4096], P(None, 'dp', 'fsdp')
- mixed: bfloat16 [4096, 4096], P('dp', 'fsdp')
Inputs may be any that keep to these rules, and one draw needn't show every extreme that they name: `counts`: at most 512, reached on some index of dp in every draw.
All inputs are finite; a program needn't handle non-finite values.
Results may differ from a plain program's by a relative error of at most 0.0095.
Values may be sent and summed in bfloat16 or wider, within the bound.
A program may use at most 192 MiB of HBM per device.

v0:
```python
import jax
import jax.numpy as jnp
from jax import lax
from jax.sharding import PartitionSpec as P

D = 4096
LAYERS = 4
GRID = 16
STEP = 40
beta_one = 0.9
beta_two = 0.95
adam_eps = 1e-08
learning_rate = 0.0024
weight_decay = 0.05
norm_eps = 1e-06


def position_code(patch_index):
    quarter = D // 4
    freqs = 1.0 / 10000.0 ** (jnp.arange(quarter, dtype=jnp.float32) / quarter)
    across = (patch_index // GRID).astype(jnp.float32)[:, None] * freqs[None, :]
    downward = (patch_index % GRID).astype(jnp.float32)[:, None] * freqs[None, :]
    return jnp.concatenate(
        [jnp.sin(across), jnp.cos(across), jnp.sin(downward), jnp.cos(downward)], axis=1
    )


def layer_norm(stream, gain_row):
    centre = jnp.mean(stream, axis=1, keepdims=True)
    shifted = stream - centre
    spread = jnp.mean(shifted * shifted, axis=1, keepdims=True)
    return (shifted * lax.rsqrt(spread + norm_eps) * gain_row[None, :]).astype(jnp.bfloat16)


def adam_update(params, moments, seconds, gradients, factor):
    clipped = gradients * factor
    moments_new = beta_one * moments + (1.0 - beta_one) * clipped
    seconds_new = beta_two * seconds + (1.0 - beta_two) * clipped * clipped
    direction = (
        moments_new
        / (1.0 - beta_one**STEP)
        / (jnp.sqrt(seconds_new / (1.0 - beta_two**STEP)) + adam_eps)
    )
    params_new = params - learning_rate * (direction + weight_decay * params)
    return (params_new, moments_new, seconds_new)


def advance(stream, branch, current, col_first, col_count):
    if current + 1 < LAYERS:
        widened = lax.all_gather(branch, "fsdp", axis=1, tiled=True)
        return stream + widened.astype(jnp.float32)
    return lax.dynamic_slice_in_dim(stream, col_first, col_count, 1) + branch.astype(jnp.float32)


def per_device(
    tokens, counts, patch_index, clip_limit, norm_gain, params, moments, seconds, gradients
):
    squares = lax.psum(jnp.sum(gradients * gradients), ("dp", "fsdp"))
    factor = jnp.minimum(1.0, clip_limit / (jnp.sqrt(squares) + 1e-06))
    params_new, moments_new, seconds_new = adam_update(params, moments, seconds, gradients, factor)
    weights = params_new.astype(jnp.bfloat16)
    tok_rows = tokens.shape[0]
    col_count = weights.shape[2]
    col_first = lax.axis_index("fsdp") * col_count
    valid = lax.broadcasted_iota(jnp.int32, (tok_rows, 1), 0) < counts[0]
    stream = jnp.where(valid, tokens.astype(jnp.float32) + position_code(patch_index), 0.0)
    gathered = lax.all_gather(weights, "dp", axis=1, tiled=True)
    for current in range(LAYERS):
        normed = layer_norm(stream, norm_gain[current])
        branch = jnp.dot(normed, gathered[current], preferred_element_type=jnp.float32).astype(
            jnp.bfloat16
        )
        stream = advance(stream, branch, current, col_first, col_count)
    mixed = jnp.where(valid, stream, 0.0).astype(jnp.bfloat16)
    return (params_new, moments_new, seconds_new, mixed)


def solution(mesh):
    in_specs = (
        P("dp", None),
        P("dp"),
        P("dp"),
        P(),
        P(),
        P(None, "dp", "fsdp"),
        P(None, "dp", "fsdp"),
        P(None, "dp", "fsdp"),
        P(None, "dp", "fsdp"),
    )
    out_specs = (
        P(None, "dp", "fsdp"),
        P(None, "dp", "fsdp"),
        P(None, "dp", "fsdp"),
        P("dp", "fsdp"),
    )
    return jax.shard_map(
        per_device, mesh=mesh, in_specs=in_specs, out_specs=out_specs, check_vma=False
    )
```

profile of v0, /device:TPU:0, one launch (start us, length us, event | category | flops | bytes accessed | tf_op | source)
XLA Modules:
  0.0 556.9 jit_solution(18285389573598532073)
XLA Ops:
  7.2 6.1 %multiply_reduce_fusion.4 = f32[]{:T(128)} fusion(f32[4,512,1024]{2,1,0:T(8,128)} %param.17), kind=kLoop, calls=%fused_computation.25 | loop fusion | flops 4194303 | bytes 8388612 | tf_op jit(solution)/shard_map/reduce_sum | solution.py:58
  14.0 42.2 %psum.7 = f32[]{:T(128)} all-reduce(f32[]{:T(128)} %multiply_reduce_fusion.4), channel_id=1, replica_groups=mesh['dp'=8,'fsdp'=4] {'dp','fsdp'}, use_global_device_ids=true, to_apply=%region_1.0 | all-reduce | flops 1 | bytes 8 | tf_op jit(solution)/shard_map/psum | solution.py:58
  57.0 20.8 %fusion.30 = (bf16[4,512,1024]{2,1,0:T(8,128)(2,1)}, f32[4,512,1024]{2,1,0:T(8,128)}, f32[4,512,1024]{2,1,0:T(8,128)}, f32[4,512,1024]{2,1,0:T(8,128)}) fusion(f32[4,512,1024]{2,1,0:T(8,128)} %param.14, f32[4,512,1024]{2,1,0:T(8,128)} %param.17, f32[]{:T(128)S(6)} %min.3, f32[4,512,1024]{2,1,0:T(8,128)} %param.15, f32[4,512,1024]{2,1,0:T(8,128)} %param.16), kind=kLoop, calls=%fused_computation.71 | loop fusion | flops 35651584 | bytes 62914564 | tf_op jit(solution)/shard_map/convert_element_type | solution.py:61
  77.8 0.2 all-gather.7.cloned.1.call-start
  78.9 14.7 %multiply_sine_fusion.1 = (f32[512,1024]{1,0:T(8,128)S(1)}, f32[512,1024]{1,0:T(8,128)S(1)}, f32[512,1024]{1,0:T(8,128)S(1)}, f32[512,1024]{1,0:T(8,128)S(1)}) fusion(f32[1024]{0:T(1024)S(1)} %negate_power_fusion, f32[512]{0:T(512)S(1)} %get-tuple-element.24, f32[512]{0:T(512)S(1)} %get-tuple-element.25), kind=kLoop, calls=%fused_computation.41 | loop fusion | flops 1048576 | bytes 8396800 | tf_op jit(solution)/shard_map/sin | solution.py:24
  93.7 1.7 fusion.28
  95.4 3.2 copy-done
  98.6 1.0 multiply_reduce_fusion.3
  99.6 139.0 %all-gather.5.cloned.1.call-done = bf16[4,4096,1024]{2,1,0:T(8,128)(2,1)} async-done(((bf16[4,512,1024]{2,1,0:T(8,128)(2,1)}), bf16[4,4096,1024]{2,1,0:T(8,128)(2,1)}) %all-gather.5.cloned.1.call-update) | async-done | bytes 33554448 | tf_op jit(solution)/shard_map/all_gather | solution.py:67
  238.6 11.3 %fusion.18 = bf16[512,1024]{1,0:T(8,128)(2,1)} fusion(bf16[4,4096,1024]{2,1,0:T(8,128)(2,1)} %all-gather.5.cloned.1.call-done, f32[512,4096]{1,0:T(8,128)} %copy-done, f32[4096]{0:T(1024)S(1)} %bitcast.33, f32[512]{0:T(512)S(1)} %add_rsqrt_fusion.3, f32[512]{0:T(512)S(1)} %broadcast_multiply_fusion.3), kind=kOutput, calls=%fused_computation.43 | convolution fusion | flops 4303880192 | bytes 17846272 | tf_op jit(solution)/shard_map/dot_general | solution.py:70
  250.0 80.8 %all-gather.7.cloned.1.call-done = bf16[512,4096]{1,0:T(8,128)(2,1)} async-done(((bf16[512,1024]{1,0:T(8,128)(2,1)}), bf16[512,4096]{1,0:T(8,128)(2,1)}) %all-gather.7.cloned.1.call-update) | async-done | bytes 4194320 | tf_op jit(solution)/shard_map/all_gather | solution.py:50
  330.8 5.6 %fusion.22 = f32[512]{0:T(512)S(1)} fusion(f32[512,4096]{1,0:T(8,128)} %copy-done, bf16[512,4096]{1,0:T(8,128)(2,1)} %all-gather.7.cloned.1.call-done), kind=kLoop, calls=%fused_computation.47 | loop fusion | flops 6290944 | bytes 12584960 | tf_op jit(solution)/shard_map/reduce_sum | solution.py:29
  336.6 5.2 multiply_reduce_fusion.2
  341.8 9.2 %fusion.19 = bf16[512,1024]{1,0:T(8,128)(2,1)} fusion(bf16[4,4096,1024]{2,1,0:T(8,128)(2,1)} %all-gather.5.cloned.1.call-done, f32[4096]{0:T(1024)S(1)} %bitcast.32, f32[512]{0:T(512)S(1)} %add_rsqrt_fusion.2, f32[512]{0:T(512)S(1)} %broadcast_multiply_fusion.2, f32[512,4096]{1,0:T(8,128)S(1)} %bitcast.29, bf16[512,4096]{1,0:T(8,128)(2,1)S(1)} %copy-done.2), kind=kOutput, calls=%fused_computation.44 | convolution fusion | flops 4308074496 | bytes 22040576 | tf_op jit(solution)/shard_map/dot_general | solution.py:70
  351.1 0.3 all-gather.11.cloned.1.call-start
  351.4 79.1 %all-gather.9.cloned.1.call-done = bf16[512,4096]{1,0:T(8,128)(2,1)} async-done(((bf16[512,1024]{1,0:T(8,128)(2,1)}), bf16[512,4096]{1,0:T(8,128)(2,1)}) %all-gather.9.cloned.1.call-update) | async-done | bytes 4194320 | tf_op jit(solution)/shard_map/all_gather | solution.py:50
  430.4 10.3 %fusion.27 = (f32[512]{0:T(512)S(1)}, f32[512,4096]{1,0:T(8,128)}) fusion(bf16[512,4096]{1,0:T(8,128)(2,1)} %all-gather.9.cloned.1.call-done, f32[512,4096]{1,0:T(8,128)} %copy-done, bf16[512,4096]{1,0:T(8,128)(2,1)} %all-gather.7.cloned.1.call-done), kind=kLoop, calls=%fused_computation.69 | loop fusion | flops 10485248 | bytes 25167872 | tf_op jit(solution)/shard_map/reduce_sum | solution.py:29
  440.8 4.5 multiply_reduce_fusion.1
  445.3 1.3 copy-done.1
  446.5 9.0 %fusion.20 = bf16[512,1024]{1,0:T(8,128)(2,1)} fusion(bf16[4,4096,1024]{2,1,0:T(8,128)(2,1)} %all-gather.5.cloned.1.call-done, f32[512,4096]{1,0:T(8,128)S(1)} %copy-done.1, f32[4096]{0:T(1024)S(1)} %bitcast.31, f32[512]{0:T(512)S(1)} %add_rsqrt_fusion.1, f32[512]{0:T(512)S(1)} %broadcast_multiply_fusion.1), kind=kOutput, calls=%fused_computation.45 | convolution fusion | flops 4303880192 | bytes 17846272 | tf_op jit(solution)/shard_map/dot_general | solution.py:70
  455.6 79.4 %all-gather.11.cloned.1.call-done = bf16[512,4096]{1,0:T(8,128)(2,1)} async-done(((bf16[512,1024]{1,0:T(8,128)(2,1)}), bf16[512,4096]{1,0:T(8,128)(2,1)}) %all-gather.11.cloned.1.call-update) | async-done | bytes 4194320 | tf_op jit(solution)/shard_map/all_gather | solution.py:50
  535.0 5.5 fusion.26
  540.5 1.0 multiply_reduce_fusion
  541.4 8.9 %select_convert_fusion = bf16[512,1024]{1,0:T(8,128)(2,1)} fusion(f32[512,4096]{1,0:T(8,128)S(1)} %get-tuple-element.5, s32[]{:T(128)S(6)} %select_n.26, bf16[4,4096,1024]{2,1,0:T(8,128)(2,1)} %all-gather.5.cloned.1.call-done, f32[4096]{0:T(1024)S(1)} %bitcast.30, f32[512]{0:T(512)S(1)} %add_rsqrt_fusion, f32[512]{0:T(512)S(1)} %broadcast_multiply_fusion, ...), kind=kOutput, calls=%fused_computation.42 | convolution fusion | flops 4305977344 | bytes 19943940 | tf_op jit(solution)/shard_map/dot_general | solution.py:70
  (33 shorter events, 0.4 us)
Async XLA Ops:
  7.2 231.5 %all-gather.5.cloned.1.call-start = ((), (), s32[]{:S(2)}) async-start(), calls=%async_computation | async-start | bytes 37748736 | tf_op jit(solution)/shard_map/all_gather | solution.py:67
  57.0 21.9 %copy-start.5 = (s32[512]{0:T(512)S(1)}, s32[512]{0:T(512)}, u32[]{:S(2)}) copy-start(s32[512]{0:T(512)} %param.11) | copy-start | bytes 6148
  77.8 253.0 %all-gather.7.cloned.1.call-start = ((), (), s32[]{:S(2)}) async-start(), calls=%async_computation.1 | async-start | bytes 5242880 | tf_op jit(solution)/shard_map/all_gather | solution.py:50
  78.0 15.6 %copy-start.3 = (bf16[512,4096]{1,0:T(8,128)(2,1)S(1)}, bf16[512,4096]{1,0:T(8,128)(2,1)}, u32[]{:S(2)}) copy-start(bf16[512,4096]{1,0:T(8,128)(2,1)} %param.9) | copy-start | bytes 12582916
  95.4 3.2 copy-start
  95.4 4.2 copy-start.4
  249.9 180.5 %all-gather.9.cloned.1.call-start = ((), (), s32[]{:S(2)}) async-start(), calls=%async_computation.2 | async-start | bytes 5242880 | tf_op jit(solution)/shard_map/all_gather | solution.py:50
  330.8 5.8 %copy-start.2 = (bf16[512,4096]{1,0:T(8,128)(2,1)S(1)}, bf16[512,4096]{1,0:T(8,128)(2,1)}, u32[]{:S(2)}) copy-start(bf16[512,4096]{1,0:T(8,128)(2,1)} %all-gather.7.cloned.1.call-done) | copy-start | bytes 12582916
  330.8 11.0 %slice-start = ((s8[8388608]{0:T(1024)(128)(4,1)}), s8[4194304]{0:T(1024)(128)(4,1)S(1)}, s32[]{:S(2)}) async-start(s8[8388608]{0:T(1024)(128)(4,1)} %bitcast.28), calls=%async_computation.4 | async-start | bytes 8388608
  336.6 5.2 slice-start.1
  351.1 183.9 %all-gather.11.cloned.1.call-start = ((), (), s32[]{:S(2)}) async-start(), calls=%async_computation.3 | async-start | bytes 5242880 | tf_op jit(solution)/shard_map/all_gather | solution.py:50
  440.7 5.8 %copy-start.1 = (f32[512,4096]{1,0:T(8,128)S(1)}, f32[512,4096]{1,0:T(8,128)}, u32[]{:S(2)}) copy-start(f32[512,4096]{1,0:T(8,128)} %get-tuple-element.7) | copy-start | bytes 25165828
Sparse Core Ops, SparseCore 0:
  77.9 160.6 all-gather.4
  250.0 80.7 all-gather.6
  351.2 79.2 all-gather.8
  455.7 79.2 all-gather.10
where the time goes:
time: 557 us
  waiting for transfers between devices  378 us (68%)
  other arithmetic  76.5 us (14%)
  blocking collectives  42.2 us (8%)
  matrix products  38.4 us (7%)
  between operations  16.1 us (3%)
    all_gather x3, waiting for transfers between devices, advance(): widened = lax.all_gather(branch, 'fsdp', axis=1, tiled=True)  239 us
    all_gather x1, waiting for transfers between devices, per_device(): gathered = lax.all_gather(weights, 'dp', axis=1, tiled=True)  139 us
    psum x1, blocking collectives, per_device(): squares = lax.psum(jnp.sum(gradients * gradients), ('dp', 'fsdp'))  42.2 us
    dot_general x4, matrix products, per_device(): jnp.dot(normed, gathered[current], preferred_element_type=jnp.float32)  38.4 us
    reduce_sum x4, other arithmetic, layer_norm(): centre = jnp.mean(stream, axis=1, keepdims=True)  23.1 us
    convert_element_type x1, other arithmetic, per_device(): weights = params_new.astype(jnp.bfloat16)  20.8 us
    sin x1, other arithmetic, position_code(): jnp.sin(across)  14.7 us
    reduce_sum x4, other arithmetic, layer_norm(): spread = jnp.mean(shifted * shifted, axis=1, keepdims=True)  11.6 us
  transfers between devices with their start and end apart: 4, of which 4 were waited for; matrix products, arithmetic and copies ran while one was open for 3% of the time, Pallas kernels for 0%

commit v1 on v0

--- a/solution.py
+++ b/solution.py
@@ -64,7 +64,12 @@
     col_first = lax.axis_index("fsdp") * col_count
     valid = lax.broadcasted_iota(jnp.int32, (tok_rows, 1), 0) < counts[0]
     stream = jnp.where(valid, tokens.astype(jnp.float32) + position_code(patch_index), 0.0)
-    gathered = lax.all_gather(weights, "dp", axis=1, tiled=True)
+    ring = [weights]
+    for hop in range(7):
+        ring.append(lax.ppermute(ring[-1], "dp", [(dev, (dev + 1) % 8) for dev in range(8)]))
+    gathered = jnp.roll(
+        jnp.concatenate(ring[::-1], axis=1), (lax.axis_index("dp") + 1) * ring[0].shape[1], axis=1
+    )
     for current in range(LAYERS):
         normed = layer_norm(stream, norm_gain[current])
         branch = jnp.dot(normed, gathered[current], preferred_element_type=jnp.float32).astype(

time: 557 us -> 802 us (1.44)
  waiting for transfers between devices: 378 us -> 564 us
  local copies, waits for them, and re-layouts: 4.64 us -> 65.8 us
    ppermute x0 -> x7, waiting for transfers between devices: none -> 324 us  [per_device(): lax.ppermute(ring[-1], 'dp', [(dev, (dev + 1) % 8) for dev in range(8)])]
    all_gather x1 -> x0, waiting for transfers between devices: 139 us -> none  [per_device(): gathered = lax.all_gather(weights, 'dp', axis=1, tiled=True)]
    unnamed x16 -> x51, local copies, waits for them, and re-layouts: 4.59 us -> 63.2 us
  transfers between devices with their start and end apart: 4 -> 10, of which waited for: 4 -> 10; matrix products, arithmetic and copies ran while one was open for 3% -> 2% of each run, Pallas kernels for 0% -> 0%
where the time goes in v1:
time: 802 us; the launch traced here: 798 us
  waiting for transfers between devices  564 us (70%)
  other arithmetic  72.9 us (9%)
  local copies, waits for them, and re-layouts  65.8 us (8%)
  blocking collectives  42.2 us (5%)
  matrix products  36.4 us (5%)
  between operations  16.2 us (2%)
    ppermute x7, waiting for transfers between devices, per_device(): lax.ppermute(ring[-1], 'dp', [(dev, (dev + 1) % 8) for dev in range(8)])  324 us
    all_gather x3, waiting for transfers between devices, advance(): widened = lax.all_gather(branch, 'fsdp', axis=1, tiled=True)  240 us
    unnamed x51, local copies, waits for them, and re-layouts  63.2 us
    psum x1, blocking collectives, per_device(): squares = lax.psum(jnp.sum(gradients * gradients), ('dp', 'fsdp'))  42.2 us
    dot_general x4, matrix products, per_device(): jnp.dot(normed, gathered[current], preferred_element_type=jnp.float32)  36.4 us
    reduce_sum x4, other arithmetic, layer_norm(): centre = jnp.mean(stream, axis=1, keepdims=True)  23.2 us
    convert_element_type x1, other arithmetic, per_device(): weights = params_new.astype(jnp.bfloat16)  20.8 us
  transfers between devices with their start and end apart: 10, of which 10 were waited for; matrix products, arithmetic and copies ran while one was open for 2% of the time, Pallas kernels for 0%

profile of v1, /device:TPU:0, one launch (start us, length us, event | category | flops | bytes accessed | tf_op | source)
XLA Modules:
  0.0 797.9 jit_solution(2472035535628997644)
XLA Ops:
  7.2 6.1 multiply_reduce_fusion.4
  14.0 42.2 %psum.7 = f32[]{:T(128)} all-reduce(f32[]{:T(128)} %multiply_reduce_fusion.4), channel_id=1, replica_groups=mesh['dp'=8,'fsdp'=4] {'dp','fsdp'}, use_global_device_ids=true, to_apply=%region_1.0 | all-reduce | flops 1 | bytes 8 | tf_op jit(solution)/shard_map/psum | solution.py:58
  57.0 20.8 %fusion.34 = (bf16[4,512,1024]{2,1,0:T(8,128)(2,1)}, f32[4,512,1024]{2,1,0:T(8,128)}, f32[4,512,1024]{2,1,0:T(8,128)}, f32[4,512,1024]{2,1,0:T(8,128)}) fusion(f32[4,512,1024]{2,1,0:T(8,128)} %param.14, f32[4,512,1024]{2,1,0:T(8,128)} %param.17, f32[]{:T(128)S(6)} %min.3, f32[4,512,1024]{2,1,0:T(8,128)} %param.15, f32[4,512,1024]{2,1,0:T(8,128)} %param.16), kind=kLoop, calls=%fused_computation.91 | loop fusion | flops 35651584 | bytes 62914564 | tf_op jit(solution)/shard_map/convert_element_type | solution.py:61
  77.8 49.0 %collective-permute-done = bf16[4,512,1024]{2,1,0:T(8,128)(2,1)S(1)} collective-permute-done((bf16[4,512,1024]{2,1,0:T(8,128)(2,1)}, bf16[4,512,1024]{2,1,0:T(8,128)(2,1)S(1)}, u32[]{:S(2)}, u32[]{:S(2)}) %collective-permute-start) | collective-permute-done | bytes 4194336 | tf_op jit(solution)/shard_map/ppermute | solution.py:69
  128.9 48.8 %collective-permute-done.1 = bf16[4,512,1024]{2,1,0:T(8,128)(2,1)S(1)} collective-permute-done((bf16[4,512,1024]{2,1,0:T(8,128)(2,1)S(1)}, bf16[4,512,1024]{2,1,0:T(8,128)(2,1)S(1)}, u32[]{:S(2)}, u32[]{:S(2)}) %collective-permute-start.1) | collective-permute-done | bytes 4194336 | tf_op jit(solution)/shard_map/ppermute | solution.py:69
  179.7 48.8 %collective-permute-done.2 = bf16[4,512,1024]{2,1,0:T(8,128)(2,1)S(1)} collective-permute-done((bf16[4,512,1024]{2,1,0:T(8,128)(2,1)S(1)}, bf16[4,512,1024]{2,1,0:T(8,128)(2,1)S(1)}, u32[]{:S(2)}, u32[]{:S(2)}) %collective-permute-start.2) | collective-permute-done | bytes 4194336 | tf_op jit(solution)/shard_map/ppermute | solution.py:69
  230.4 48.8 %collective-permute-done.3 = bf16[4,512,1024]{2,1,0:T(8,128)(2,1)S(1)} collective-permute-done((bf16[4,512,1024]{2,1,0:T(8,128)(2,1)S(1)}, bf16[4,512,1024]{2,1,0:T(8,128)(2,1)S(1)}, u32[]{:S(2)}, u32[]{:S(2)}) %collective-permute-start.3) | collective-permute-done | bytes 4194336 | tf_op jit(solution)/shard_map/ppermute | solution.py:69
  281.3 48.8 %collective-permute-done.4 = bf16[4,512,1024]{2,1,0:T(8,128)(2,1)S(1)} collective-permute-done((bf16[4,512,1024]{2,1,0:T(8,128)(2,1)S(1)}, bf16[4,512,1024]{2,1,0:T(8,128)(2,1)S(1)}, u32[]{:S(2)}, u32[]{:S(2)}) %collective-permute-start.4) | collective-permute-done | bytes 4194336 | tf_op jit(solution)/shard_map/ppermute | solution.py:69
  332.2 48.9 %collective-permute-done.5 = bf16[4,512,1024]{2,1,0:T(8,128)(2,1)} collective-permute-done((bf16[4,512,1024]{2,1,0:T(8,128)(2,1)S(1)}, bf16[4,512,1024]{2,1,0:T(8,128)(2,1)}, u32[]{:S(2)}, u32[]{:S(2)}) %collective-permute-start.5) | collective-permute-done | bytes 4194336 | tf_op jit(solution)/shard_map/ppermute | solution.py:69
  382.3 14.7 %multiply_sine_fusion.1 = (f32[512,1024]{1,0:T(8,128)S(1)}, f32[512,1024]{1,0:T(8,128)S(1)}, f32[512,1024]{1,0:T(8,128)S(1)}, f32[512,1024]{1,0:T(8,128)S(1)}) fusion(f32[1024]{0:T(1024)S(1)} %negate_power_fusion, f32[512]{0:T(512)S(1)} %get-tuple-element.24, f32[512]{0:T(512)S(1)} %get-tuple-element.25), kind=kLoop, calls=%fused_computation.41 | loop fusion | flops 1048576 | bytes 8396800 | tf_op jit(solution)/shard_map/sin | solution.py:24
  399.8 30.9 %collective-permute-done.6 = bf16[4,512,1024]{2,1,0:T(8,128)(2,1)} collective-permute-done((bf16[4,512,1024]{2,1,0:T(8,128)(2,1)}, bf16[4,512,1024]{2,1,0:T(8,128)(2,1)}, u32[]{:S(2)}, u32[]{:S(2)}) %collective-permute-start.6) | collective-permute-done | bytes 4194336 | tf_op jit(solution)/shard_map/ppermute | solution.py:69
  435.3 4.9 constant_dynamic-update-slice_fusion.14
  455.8 4.8 constant_dynamic-update-slice_fusion.7
  460.6 4.8 constant_dynamic-update-slice_fusion.6
  482.7 9.3 %fusion.18 = bf16[512,1024]{1,0:T(8,128)(2,1)} fusion(bf16[4,8192,1024]{2,1,0:T(8,128)(2,1)} %constant_dynamic-update-slice_fusion, s32[]{:T(128)S(6)} %select_n.39, f32[512,4096]{1,0:T(8,128)S(1)} %get-tuple-element.9, f32[4096]{0:T(1024)S(1)} %bitcast.31, f32[512]{0:T(512)S(1)} %add_rsqrt_fusion.3, f32[512]{0:T(512)S(1)} %broadcast_multiply_fusion.3), kind=kOutput, calls=%fused_computation.43 | convolution fusion | flops 4303880192 | bytes 17846276 | tf_op jit(solution)/shard_map/dot_general | solution.py:75
  492.0 80.8 %all-gather.4.cloned.1.call-done = bf16[512,4096]{1,0:T(8,128)(2,1)} async-done(((bf16[512,1024]{1,0:T(8,128)(2,1)}), bf16[512,4096]{1,0:T(8,128)(2,1)}) %all-gather.4.cloned.1.call-update) | async-done | bytes 4194320 | tf_op jit(solution)/shard_map/all_gather | solution.py:50
  572.9 5.6 fusion.22
  582.5 9.2 %fusion.19 = bf16[512,1024]{1,0:T(8,128)(2,1)} fusion(bf16[4,8192,1024]{2,1,0:T(8,128)(2,1)} %constant_dynamic-update-slice_fusion, s32[]{:T(128)S(6)} %add.110, s32[]{:T(128)S(6)} %select_n.39, f32[4096]{0:T(1024)S(1)} %bitcast.30, f32[512]{0:T(512)S(1)} %add_rsqrt_fusion.2, f32[512]{0:T(512)S(1)} %broadcast_multiply_fusion.2, ...), kind=kOutput, calls=%fused_computation.44 | convolution fusion | flops 4308074496 | bytes 22040584 | tf_op jit(solution)/shard_map/dot_general | solution.py:75
  591.8 79.3 %all-gather.6.cloned.1.call-done = bf16[512,4096]{1,0:T(8,128)(2,1)} async-done(((bf16[512,1024]{1,0:T(8,128)(2,1)}), bf16[512,4096]{1,0:T(8,128)(2,1)}) %all-gather.6.cloned.1.call-update) | async-done | bytes 4194320 | tf_op jit(solution)/shard_map/all_gather | solution.py:50
  671.1 10.4 %fusion.31 = (f32[512]{0:T(512)S(1)}, f32[512,4096]{1,0:T(8,128)}) fusion(bf16[512,4096]{1,0:T(8,128)(2,1)} %all-gather.6.cloned.1.call-done, f32[512,4096]{1,0:T(8,128)} %copy-done, bf16[512,4096]{1,0:T(8,128)(2,1)} %all-gather.4.cloned.1.call-done), kind=kLoop, calls=%fused_computation.89 | loop fusion | flops 10485248 | bytes 25167872 | tf_op jit(solution)/shard_map/reduce_sum | solution.py:29
  687.3 9.0 %fusion.20 = bf16[512,1024]{1,0:T(8,128)(2,1)} fusion(bf16[4,8192,1024]{2,1,0:T(8,128)(2,1)} %constant_dynamic-update-slice_fusion, s32[]{:T(128)S(6)} %add.111, s32[]{:T(128)S(6)} %select_n.39, f32[512,4096]{1,0:T(8,128)S(1)} %copy-done.2, f32[4096]{0:T(1024)S(1)} %bitcast.29, f32[512]{0:T(512)S(1)} %add_rsqrt_fusion.1, f32[512]{0:T(512)S(1)} %broadcast_multiply_fusion.1), kind=kOutput, calls=%fused_computation.45 | convolution fusion | flops 4303880192 | bytes 17846280 | tf_op jit(solution)/shard_map/dot_general | solution.py:75
  696.4 79.4 %all-gather.8.cloned.1.call-done = bf16[512,4096]{1,0:T(8,128)(2,1)} async-done(((bf16[512,1024]{1,0:T(8,128)(2,1)}), bf16[512,4096]{1,0:T(8,128)(2,1)}) %all-gather.8.cloned.1.call-update) | async-done | bytes 4194320 | tf_op jit(solution)/shard_map/all_gather | solution.py:50
  775.8 5.5 fusion.30
  782.2 8.9 %select_convert_fusion = bf16[512,1024]{1,0:T(8,128)(2,1)} fusion(f32[512,4096]{1,0:T(8,128)S(1)} %get-tuple-element.5, s32[]{:T(128)S(6)} %select_n.40, bf16[4,8192,1024]{2,1,0:T(8,128)(2,1)} %constant_dynamic-update-slice_fusion, s32[]{:T(128)S(6)} %add.112, s32[]{:T(128)S(6)} %select_n.39, f32[4096]{0:T(1024)S(1)} %bitcast.28, ...), kind=kOutput, calls=%fused_computation.42 | convolution fusion | flops 4305977344 | bytes 19943948 | tf_op jit(solution)/shard_map/dot_general | solution.py:75
  (79 shorter events, 61.6 us)
Async XLA Ops:
  7.2 565.7 %all-gather.4.cloned.1.call-start = ((), (), s32[]{:S(2)}) async-start(), calls=%async_computation | async-start | bytes 5242880 | tf_op jit(solution)/shard_map/all_gather | solution.py:50
  57.0 325.3 %copy-start.17 = (s32[512]{0:T(512)S(1)}, s32[512]{0:T(512)}, u32[]{:S(2)}) copy-start(s32[512]{0:T(512)} %param.11) | copy-start | bytes 6148
  77.8 49.0 %collective-permute-start = (bf16[4,512,1024]{2,1,0:T(8,128)(2,1)}, bf16[4,512,1024]{2,1,0:T(8,128)(2,1)S(1)}, u32[]{:S(2)}, u32[]{:S(2)}) collective-permute-start(bf16[4,512,1024]{2,1,0:T(8,128)(2,1)} %get-tuple-element.10), channel_id=1, source_target_pairs={{0,4},{4,8},{8,12},{12,16},{16,20},{20,24},{24,28},{28,0},{1,5},{5... | collective-permute-start | bytes 12582920 | tf_op jit(solution)/shard_map/ppermute | solution.py:69
  128.8 48.8 %collective-permute-start.1 = (bf16[4,512,1024]{2,1,0:T(8,128)(2,1)S(1)}, bf16[4,512,1024]{2,1,0:T(8,128)(2,1)S(1)}, u32[]{:S(2)}, u32[]{:S(2)}) collective-permute-start(bf16[4,512,1024]{2,1,0:T(8,128)(2,1)S(1)} %collective-permute-done), channel_id=1, source_target_pairs={{0,4},{4,8},{8,12},{12,16},{16,20},{20,24},{24,28},{28,0},{1,5},{5... | collective-permute-start | bytes 12582920 | tf_op jit(solution)/shard_map/ppermute | solution.py:69
  179.7 48.8 %collective-permute-start.2 = (bf16[4,512,1024]{2,1,0:T(8,128)(2,1)S(1)}, bf16[4,512,1024]{2,1,0:T(8,128)(2,1)S(1)}, u32[]{:S(2)}, u32[]{:S(2)}) collective-permute-start(bf16[4,512,1024]{2,1,0:T(8,128)(2,1)S(1)} %collective-permute-done.1), channel_id=1, source_target_pairs={{0,4},{4,8},{8,12},{12,16},{16,20},{20,24},{24,28},{28,0},{1,5},{5... | collective-permute-start | bytes 12582920 | tf_op jit(solution)/shard_map/ppermute | solution.py:69
  230.4 48.8 %collective-permute-start.3 = (bf16[4,512,1024]{2,1,0:T(8,128)(2,1)S(1)}, bf16[4,512,1024]{2,1,0:T(8,128)(2,1)S(1)}, u32[]{:S(2)}, u32[]{:S(2)}) collective-permute-start(bf16[4,512,1024]{2,1,0:T(8,128)(2,1)S(1)} %collective-permute-done.2), channel_id=1, source_target_pairs={{0,4},{4,8},{8,12},{12,16},{16,20},{20,24},{24,28},{28,0},{1,5},{5... | collective-permute-start | bytes 12582920 | tf_op jit(solution)/shard_map/ppermute | solution.py:69
  279.3 2.1 copy-start.11
  281.3 48.8 %collective-permute-start.4 = (bf16[4,512,1024]{2,1,0:T(8,128)(2,1)S(1)}, bf16[4,512,1024]{2,1,0:T(8,128)(2,1)S(1)}, u32[]{:S(2)}, u32[]{:S(2)}) collective-permute-start(bf16[4,512,1024]{2,1,0:T(8,128)(2,1)S(1)} %collective-permute-done.3), channel_id=1, source_target_pairs={{0,4},{4,8},{8,12},{12,16},{16,20},{20,24},{24,28},{28,0},{1,5},{5... | collective-permute-start | bytes 12582920 | tf_op jit(solution)/shard_map/ppermute | solution.py:69
  330.2 2.0 copy-start.13
  332.2 48.9 %collective-permute-start.5 = (bf16[4,512,1024]{2,1,0:T(8,128)(2,1)S(1)}, bf16[4,512,1024]{2,1,0:T(8,128)(2,1)}, u32[]{:S(2)}, u32[]{:S(2)}) collective-permute-start(bf16[4,512,1024]{2,1,0:T(8,128)(2,1)S(1)} %collective-permute-done.4), channel_id=1, source_target_pairs={{0,4},{4,8},{8,12},{12,16},{16,20},{20,24},{24,28},{28,0},{1,5},{5... | collective-permute-start | bytes 12582920 | tf_op jit(solution)/shard_map/ppermute | solution.py:69
  381.1 49.6 %collective-permute-start.6 = (bf16[4,512,1024]{2,1,0:T(8,128)(2,1)}, bf16[4,512,1024]{2,1,0:T(8,128)(2,1)}, u32[]{:S(2)}, u32[]{:S(2)}) collective-permute-start(bf16[4,512,1024]{2,1,0:T(8,128)(2,1)} %collective-permute-done.5), channel_id=1, source_target_pairs={{0,4},{4,8},{8,12},{12,16},{16,20},{20,24},{24,28},{28,0},{1,5},{5... | collective-permute-start | bytes 12582920 | tf_op jit(solution)/shard_map/ppermute | solution.py:69
  382.2 14.8 %copy-start.15 = (bf16[512,4096]{1,0:T(8,128)(2,1)S(1)}, bf16[512,4096]{1,0:T(8,128)(2,1)}, u32[]{:S(2)}) copy-start(bf16[512,4096]{1,0:T(8,128)(2,1)} %param.9) | copy-start | bytes 12582916
  398.7 84.0 %copy-start = (f32[512,4096]{1,0:T(8,128)}, f32[512,4096]{1,0:T(8,128)S(1)}, u32[]{:S(2)}) copy-start(f32[512,4096]{1,0:T(8,128)S(1)} %get-tuple-element.9) | copy-start | bytes 25165828
  399.8 40.5 %copy-start.14 = (bf16[4,512,1024]{2,1,0:T(8,128)(2,1)S(1)}, bf16[4,512,1024]{2,1,0:T(8,128)(2,1)}, u32[]{:S(2)}) copy-start(bf16[4,512,1024]{2,1,0:T(8,128)(2,1)} %copy-done.13) | copy-start | bytes 12582916
  435.3 7.5 copy-start.12
  440.3 5.3 copy-start.10
  442.9 5.3 copy-start.8
  445.6 5.2 copy-start.6
  448.2 5.1 copy-start.3
  492.0 179.1 %all-gather.6.cloned.1.call-start = ((), (), s32[]{:S(2)}) async-start(), calls=%async_computation.1 | async-start | bytes 5242880 | tf_op jit(solution)/shard_map/all_gather | solution.py:50
  572.9 7.0 copy-start.1
  572.9 8.2 %copy-start.4 = (bf16[512,4096]{1,0:T(8,128)(2,1)S(1)}, bf16[512,4096]{1,0:T(8,128)(2,1)}, u32[]{:S(2)}) copy-start(bf16[512,4096]{1,0:T(8,128)(2,1)} %all-gather.4.cloned.1.call-done) | copy-start | bytes 12582916
  591.7 184.0 %all-gather.8.cloned.1.call-start = ((), (), s32[]{:S(2)}) async-start(), calls=%async_computation.2 | async-start | bytes 5242880 | tf_op jit(solution)/shard_map/all_gather | solution.py:50
  681.5 5.8 copy-start.2
  (4 other events, 6.9 us)
Sparse Core Ops, SparseCore 0:
  492.1 80.7 all-gather.3
  591.9 79.2 all-gather.5
  696.5 79.2 all-gather.7
